TPU v7x, 512 devices: a whole 4x8x8 slice. The times are simulated.
512 devices in a mesh: exc: 8 (over z), slab: 64 (over y, x, core).
Axes of the slice: x: 4, y: 8, z: 8, core: 2. Of those that a mesh axis runs over, the one named last changes fastest.
Arguments:
- q_forward: float32 [8, 32768], P('exc', 'slab'), may hold values from -6 to 6
- q_adjoint: float32 [8, 32768], P('exc', 'slab'), may hold values from -6 to 6
- panel_offset: float32 [3, 32768], P(None, 'slab'), may hold values from -0.5 to 0.5
- block_anchor: int32 [3, 256], P(None, 'slab'), may hold values from 0 to 127, as said below
- kernel_hat: float32 [128, 128, 128], P(None, 'slab'), may hold values from 0.05 to 1, as said below
- near_list: int32 [256, 8], P('slab'), may hold values from 0 to 255, as said below
- near_count: int32 [256], P('slab'), may hold values from 1 to 8, as said below
- panel_vertices: int32 [3, 32768], P(None, 'slab'), may hold values from 0 to 16383, as said below
Outputs:
- vertex_grad: float32 [3, 16384], P(None, ('exc', 'slab'))
Inputs may be any that keep to these rules, and one draw needn't show every extreme that they name: Block i lies in the planes of slab index i // 4: block_anchor[0, i] // 2 == i // 4. Even in every dimension: kernel_hat[a, b, c] equals kernel_hat[(-a) mod 128, (-b) mod 128, (-c) mod 128]. `near_list`: every entry of a block i's list, valid or not, is a block whose slab index differs from i // 4 by -1, 0 or 1 modulo the number of slab indices. `near_count`: some block has 8 valid entries. `panel_vertices`: vertex v belongs to slab index (v // 32) mod (number of slab indices); the vertices of a panel of block i belong to slab indices that differ from i // 4 by -1, 0 or 1 modulo the number of slab indices.
All inputs are finite; a program needn't handle non-finite values.
Results may differ from a plain program's by a relative error of at most 0.0003.
Values sent between devices are 32-bit elements; how exact they have to be, the bound alone decides.
A program may use at most 192 MiB of HBM per device.

v0:
```python
import functools
import math

import jax
import jax.numpy as jnp
from jax import lax
from jax.experimental import pallas as pl
from jax.experimental.pallas import tpu as pltpu
from jax.sharding import PartitionSpec as P

G = 128
B = 128
VCH = 32
NS = 64
NE = 8
NB = 4
MAXN = 8
MESH = pl.DeviceIdType.MESH
F32 = jnp.float32
BF16 = jnp.bfloat16
soften_sq = 16.0

SIN = [(-1) ** n * (2.0 * math.pi) ** (2 * n + 1) / math.factorial(2 * n + 1) for n in range(7)]


def iota(shape, dim):
    return lax.broadcasted_iota(jnp.int32, shape, dim)


def cos_turns(t):
    w = t - jnp.floor(t + 0.5)
    z = 0.25 - jnp.abs(w)
    z2 = z * z
    p = SIN[6]
    for n in range(5, -1, -1):
        p = SIN[n] + z2 * p
    return z * p


def sin_turns(t):
    return cos_turns(t - 0.25)


def split(a):
    high = a.astype(BF16)
    return high, (a - high.astype(F32)).astype(BF16)


def dot(a, b, nt=False):
    dims = (((1,), (1 if nt else 0,)), ((), ()))
    return lax.dot_general(a, b, dims, preferred_element_type=F32)


def dot3(a, b, nt=False):
    (ah, al), (bh, bl) = a, b
    return dot(ah, bh, nt) + (dot(al, bh, nt) + dot(ah, bl, nt))


def lagrange(t):
    values = [0.5 * t * (t - 1.0), 1.0 - t * t, 0.5 * t * (t + 1.0)]
    slopes = [t - 0.5, -2.0 * t, t + 0.5]
    return values, slopes


def stencil_charges(charges, weights):
    lane = iota((8, 128), 1)
    out = jnp.zeros((8, 128), F32)
    for i in range(3):
        for j in range(3):
            part = charges * weights[0][i] * weights[1][j]
            for k in range(3):
                total = jnp.sum(part * weights[2][k], axis=1, keepdims=True)
                out = jnp.where(lane == 9 * i + 3 * j + k, total, out)
    return out


def lane_tables():
    row = iota((256, 256), 0)
    col = iota((256, 256), 1)
    half = row // 128
    field = (row % 64) // 32
    k = row % 32 % 3 - 1
    part = col // 128
    c = col % 128
    real = jnp.where(half == field, 0.0, jnp.where(half == 0, -0.25, 0.25))
    shift = real + jnp.where(part == 1, 0.25, 0.0)
    return cos_turns((c * k).astype(F32) * (1.0 / G) + shift)


def plane_of(index):
    return jnp.where(index < 64, 2 * index, 2 * index - 127)


def plane_tables():
    r = iota((128, 128), 0)
    c = iota((128, 128), 1)
    forward = (r * plane_of(c)).astype(F32) * (1.0 / G)
    back = (plane_of(r) * c).astype(F32) * (1.0 / G)
    fwd = jnp.concatenate([cos_turns(forward), sin_turns(forward)], axis=1)
    inv = jnp.concatenate([cos_turns(back), sin_turns(back)], axis=1)
    return fwd, inv


def block_phases(x, first_row):
    lane = iota((NS, 128), 1)
    rows = jnp.where(lane < 64, x[:, 28:29], x[:, 92:93])
    j = (lane % 32 // 3 % 3 - 1).astype(F32)
    lanes = []
    for b in range(2):
        t = (rows + j) * ((first_row + b).astype(F32) * (1.0 / G))
        lanes.append((cos_turns(t), sin_turns(t)))
    columns, upper = [], []
    for g in range(2):
        t = x[:, 64 * g + 29 : 64 * g + 30] * (lane.astype(F32) * (1.0 / G))
        columns.append((cos_turns(t), sin_turns(t)))
        upper.append(jnp.broadcast_to(x[:, 64 * g + 27 : 64 * g + 28], (NS, 128)) > 0.5)
    return lanes, columns, upper


def spectrum_to_partials(xs, first_row, table_ref, split_tables, plane_fwd, plane_inv, kernel_rows, roll):
    phases = [block_phases(xs[h], first_row) for h in range(2)]
    rows = []
    for b in range(2):
        for h in range(2):
            cosine, sine = phases[h][0][b]
            rows.append(jnp.concatenate([xs[h] * cosine, xs[h] * sine], axis=1))
    mixed = split(jnp.concatenate(rows, axis=0))
    planes = [[[None, None] for _ in range(4)] for _ in range(2)]

    def add(b, q, part, value):
        old = planes[b][q][part]
        planes[b][q][part] = value if old is None else old + value

    for g in range(2):
        moved = []
        for i in range(3):
            y = dot3(mixed, split_tables(g, i))
            moved.append(y)
        for b in range(2):
            for h in range(2):
                cosine, sine = phases[h][1][g]
                upper = phases[h][2][g]
                at = slice((2 * b + h) * NS, (2 * b + h + 1) * NS)
                v = []
                for i in range(3):
                    yr, yi = moved[i][at, :128], moved[i][at, 128:]
                    v.append((yr * cosine + yi * sine, yi * cosine - yr * sine))
                for part in range(2):
                    low, mid, top = (v[i][part] for i in range(3))
                    add(b, 0, part, jnp.where(upper, 0.0, low))
                    add(b, 1, part, jnp.where(upper, low, mid))
                    add(b, 2, part, jnp.where(upper, mid, top))
                    add(b, 3, part, jnp.where(upper, top, 0.0))
    left, right = [], []
    for b in range(2):
        both = []
        for part in range(2):
            even = planes[b][1][part] + roll(planes[b][3][part], 1, 0)
            odd = planes[b][2][part] + roll(planes[b][0][part], NS - 1, 0)
            both.append(jnp.concatenate([even, odd], axis=0))
        left += both
        right += [both[1], -both[0]]
    stacked = jnp.concatenate(
        [jnp.concatenate(left, axis=1), jnp.concatenate(right, axis=1)], axis=0
    )
    spectrum = dot3(plane_fwd, split(stacked))
    left, right = [], []
    for b in range(2):
        pr = spectrum[:, 256 * b : 256 * b + 128] * kernel_rows[b]
        pi = spectrum[:, 256 * b + 128 : 256 * b + 256] * kernel_rows[b]
        left += [pr, pi]
        right += [-pi, pr]
    stacked = jnp.concatenate(
        [jnp.concatenate(left, axis=1), jnp.concatenate(right, axis=1)], axis=0
    )
    back = dot3(plane_inv, split(stacked))
    levels = []
    for b in range(2):
        parts = []
        for part in range(2):
            at = slice(256 * b + 128 * part, 256 * b + 128 * part + 128)
            even, odd = back[:NS, at], back[NS:, at]
            parts.append([roll(odd, 1, 0), even, odd, roll(even, NS - 1, 0)])
        levels.append(parts)
    total = None
    for g in range(2):
        for i in range(3):
            rows = []
            for b in range(2):
                for h in range(2):
                    cosine, sine = phases[h][1][g]
                    upper = phases[h][2][g]
                    dr, di = (jnp.where(upper, levels[b][part][i + 1], levels[b][part][i]) for part in range(2))
                    rows.append(
                        jnp.concatenate([dr * cosine - di * sine, dr * sine + di * cosine], axis=1)
                    )
            value = dot3(split(jnp.concatenate(rows, axis=0)), split_tables(g, i), nt=True)
            total = value if total is None else total + value
    out = []
    for h in range(2):
        value = None
        for b in range(2):
            cosine, sine = phases[h][0][b]
            at = slice((2 * b + h) * NS, (2 * b + h + 1) * NS)
            part = total[at, :128] * cosine + total[at, 128:] * sine
            value = part if value is None else value + part
        out.append(value)
    return out


def far_rows(potential, weights, slopes):
    first = second = third = None
    for i in range(3):
        plain = turned = leaned = None
        for j in range(3):
            value = slope = None
            for k in range(3):
                at = 9 * i + 3 * j + k
                column = potential[:, at : at + 1]
                a, b = column * weights[2][k], column * slopes[2][k]
                value = a if value is None else value + a
                slope = b if slope is None else slope + b
            a, b, c = value * weights[1][j], value * slopes[1][j], slope * weights[1][j]
            plain = a if plain is None else plain + a
            turned = b if turned is None else turned + b
            leaned = c if leaned is None else leaned + c
        a, b, c = plain * slopes[0][i], turned * weights[0][i], leaned * weights[0][i]
        first = a if first is None else first + a
        second = b if second is None else second + b
        third = c if third is None else third + c
    return first, second, third


def kernel(
    qf_ref,
    qa_ref,
    offset_ref,
    anchor_ref,
    khat_ref,
    near_ref,
    count_ref,
    vertex_ref,
    out_ref,
    charge,
    swapped,
    offs,
    eight,
    message,
    near_send,
    own,
    gathered,
    near_rows,
    khat,
    table_high,
    table_low,
    partial,
    arrived,
    spread,
    near_sum,
    grad,
    owner,
    owed,
    returned,
    local_sem,
    send1,
    recv1,
    near_send_sem,
    near_recv_sem,
    send2,
    recv2,
    send3,
    recv3,
):
    e = lax.axis_index("exc")
    me = lax.axis_index("slab")
    up = lax.rem(me + 1, NS)
    down = lax.rem(me + NS - 1, NS)

    barrier = pltpu.get_barrier_semaphore()

    def greet(k, _):
        pl.semaphore_signal(
            barrier, inc=1, device_id=(e, lax.rem(me + k, NS)), device_id_type=MESH
        )
        return 0

    lax.fori_loop(1, NS, greet, 0)

    def greet_far(k, _):
        other = lax.rem(e + k, NE)
        for at in (down, me, up):
            pl.semaphore_signal(barrier, inc=1, device_id=(other, at), device_id_type=MESH)
        return 0

    lax.fori_loop(1, NE, greet_far, 0)

    kcopy = pltpu.make_async_copy(khat_ref, khat, local_sem)
    kcopy.start()

    for g in range(2):
        for h in range(2):
            m = 2 * g + h
            at = slice(128 * m, 128 * m + 128)
            for f in range(2):
                row = 4 * g + 2 * f + h
                charge[row : row + 1, :] = (qf_ref, qa_ref)[f][0:1, at]
                swapped[row : row + 1, :] = (qa_ref, qf_ref)[f][0:1, at]
                for c in range(3):
                    offs[c, row : row + 1, :] = offset_ref[c : c + 1, at]
            for c in range(3):
                place = offset_ref[c : c + 1, at] + anchor_ref[c, m].astype(F32)
                near_send[4 * c + m : 4 * c + m + 1, :] = place
                own[m, c : c + 1, :] = place
            near_send[12 + m : 13 + m, :] = qf_ref[0:1, at]
            near_send[16 + m : 17 + m, :] = qa_ref[0:1, at]
            own[m, 3:4, :] = qf_ref[0:1, at]
            own[m, 4:5, :] = qa_ref[0:1, at]
    near_send[20:24, :] = jnp.zeros((4, 128), F32)
    near_rows[1, :, :] = near_send[...]
    weights, slopes = [], []
    for c in range(3):
        w, s = lagrange(offs[c])
        weights.append(w)
        slopes.append(s)
    value = stencil_charges(charge[...], weights)
    lane = iota((8, 128), 1)
    row = iota((8, 128), 0)
    for g in range(2):
        for h in range(2):
            m = 2 * g + h
            here = row == 4 * g + h
            plane = (anchor_ref[0, m] - 2 * me).astype(F32)
            for at, number in (
                (27, plane),
                (28, anchor_ref[1, m].astype(F32)),
                (29, anchor_ref[2, m].astype(F32)),
            ):
                value = jnp.where(here & (lane == at), number, value)
    eight[...] = value
    text = eight[0:2, :]
    for t in range(1, 4):
        text = text + pltpu.roll(eight[2 * t : 2 * t + 2, :], 32 * t, 1)
    message[...] = text
    gathered[me] = text

    pl.semaphore_wait(barrier, NS - 1 + 3 * (NE - 1))

    def send_message(k, _):
        pltpu.make_async_remote_copy(
            src_ref=message,
            dst_ref=gathered.at[me],
            send_sem=send1,
            recv_sem=recv1,
            device_id=(e, lax.rem(me + k, NS)),
            device_id_type=MESH,
        ).start()
        return 0

    lax.fori_loop(1, NS, send_message, 0)
    near_up = pltpu.make_async_remote_copy(
        src_ref=near_send,
        dst_ref=near_rows.at[0],
        send_sem=near_send_sem.at[0],
        recv_sem=near_recv_sem.at[0],
        device_id=(e, up),
        device_id_type=MESH,
    )
    near_down = pltpu.make_async_remote_copy(
        src_ref=near_send,
        dst_ref=near_rows.at[2],
        send_sem=near_send_sem.at[1],
        recv_sem=near_recv_sem.at[1],
        device_id=(e, down),
        device_id_type=MESH,
    )
    near_up.start()
    near_down.start()

    base = lane_tables()
    lanes = iota((256, 256), 0) % 128
    for g in range(2):
        for i in range(3):
            mine = (lanes // 64 == g) & (lanes % 32 // 9 == i)
            high, low = split(jnp.where(mine, base, 0.0))
            table_high[3 * g + i] = high
            table_low[3 * g + i] = low
    fwd, inv = plane_tables()
    plane_fwd, plane_inv = split(fwd), split(inv)
    vertex = iota((3 * NE * VCH, 128), 0)
    for m in range(NB):
        hits = None
        for corner in range(3):
            v = vertex_ref[corner : corner + 1, 128 * m : 128 * m + 128]
            span = v // VCH
            relative = (span % NS - me + 1 + NS) % NS
            local = relative * (NE * VCH) + span // NS * VCH + v % VCH
            hit = jnp.where(vertex == local, 1.0, 0.0)
            hits = hit if hits is None else hits + hit
        owner[m] = hits.astype(BF16)

    kcopy.wait()
    kernel_rows = [khat[:, b, :] * (1.0 / (G * G * G)) for b in range(2)]
    pltpu.make_async_copy(gathered.at[pl.ds(0, NS - 1)], gathered.at[pl.ds(0, NS - 1)], recv1).wait()
    xs = [gathered[:, h, :] for h in range(2)]
    parts = spectrum_to_partials(
        xs,
        2 * me,
        None,
        lambda g, i: (table_high[3 * g + i], table_low[3 * g + i]),
        plane_fwd,
        plane_inv,
        kernel_rows,
        pltpu.roll,
    )
    for h in range(2):
        partial[:, h, :] = parts[h]
    arrived[me] = partial[me]

    def send_partial(k, _):
        to = lax.rem(me + k, NS)
        pltpu.make_async_remote_copy(
            src_ref=partial.at[to],
            dst_ref=arrived.at[me],
            send_sem=send2,
            recv_sem=recv2,
            device_id=(e, to),
            device_id_type=MESH,
        ).start()
        return 0

    lax.fori_loop(1, NS, send_partial, 0)

    near_up.wait()
    near_down.wait()
    for side in range(3):
        columns = jnp.transpose(near_rows[side])
        for q in range(5):
            for m in range(NB):
                at = 4 * q + m
                spread[4 * side + m, q] = jnp.broadcast_to(columns[:, at : at + 1], (128, 128))

    def per_block(m, _):
        mine = own[m]
        place = [mine[c : c + 1, :] for c in range(3)]
        forward, adjoint = mine[3:4, :], mine[4:5, :]

        def per_slot(slot, sums):
            other = near_ref[m, slot]
            side = jnp.minimum(lax.rem(other // NB - me + 1 + NS, NS), 2)
            index = side * NB + lax.rem(other, NB)
            keep = jnp.where(slot < count_ref[m], 1.0, 0.0).astype(F32)
            sums = list(sums)
            for chunk in range(4):
                at = pl.ds(32 * chunk, 32)
                diff = [place[c] - spread[index, c, at, :] for c in range(3)]
                square = diff[0] * diff[0] + diff[1] * diff[1] + diff[2] * diff[2]
                inverse = lax.rsqrt(square + soften_sq)
                pair = adjoint * spread[index, 3, at, :] + forward * spread[index, 4, at, :]
                weight = pair * keep * (inverse * inverse * inverse)
                for c in range(3):
                    term = diff[c] * weight
                    sums[c] = sums[c] + (
                        (term[0:8] + term[8:16]) + (term[16:24] + term[24:32])
                    )
            return tuple(sums)

        zero = jnp.zeros((8, 128), F32)
        sums = lax.fori_loop(0, MAXN, per_slot, (zero, zero, zero))
        near_sum[m] = jnp.concatenate(
            [jnp.sum(s, axis=0, keepdims=True) for s in sums] + [jnp.zeros((5, 128), F32)], axis=0
        )
        return 0

    lax.fori_loop(0, NB, per_block, 0)

    pltpu.make_async_copy(arrived.at[pl.ds(0, NS - 1)], arrived.at[pl.ds(0, NS - 1)], recv2).wait()
    potential = jnp.sum(arrived[...], axis=0)
    for t in range(4):
        turned = potential if t == 0 else pltpu.roll(potential, 128 - 32 * t, 1)
        eight[2 * t : 2 * t + 2, :] = turned
    fars = far_rows(eight[...], weights, slopes)
    grad[...] = jnp.zeros((8, NB * B), F32)
    for c in range(3):
        offs[c] = fars[c] * swapped[...]
        for g in range(2):
            for h in range(2):
                m = 2 * g + h
                at = 4 * g + h
                far = offs[c, at : at + 1, :] + offs[c, at + 2 : at + 3, :]
                grad[c : c + 1, 128 * m : 128 * m + 128] = (far - near_sum[m, c : c + 1, :]) * (
                    1.0 / (3.0 * NE)
                )
    total = None
    for m in range(NB):
        whole = grad[:, 128 * m : 128 * m + 128]
        high, rest = split(whole)
        low, last = split(whole - high.astype(F32))
        got = dot(high, owner[m], nt=True) + (dot(low, owner[m], nt=True) + dot(last, owner[m], nt=True))
        total = got if total is None else total + got
    for t in range(6):
        owed[t] = total[0:4, 128 * t : 128 * t + 128]
    returned[3 * e + 1] = owed[2 + e // 4]

    def send_owed(k, _):
        other = lax.rem(e + k, NE)
        for side, at in ((0, down), (1, me), (2, up)):

            def start():
                pltpu.make_async_remote_copy(
                    src_ref=owed.at[2 * side + other // 4],
                    dst_ref=returned.at[3 * e + side],
                    send_sem=send3,
                    recv_sem=recv3,
                    device_id=(other, at),
                    device_id_type=MESH,
                ).start()

            if side == 1:
                pl.when(k > 0)(start)
            else:
                start()
        return 0

    lax.fori_loop(0, NE, send_owed, 0)

    pltpu.make_async_copy(gathered.at[pl.ds(0, NS - 1)], gathered.at[pl.ds(0, NS - 1)], send1).wait()
    pltpu.make_async_copy(partial.at[pl.ds(0, NS - 1)], partial.at[pl.ds(0, NS - 1)], send2).wait()
    count = 3 * NE - 1
    pltpu.make_async_copy(returned.at[pl.ds(0, count)], returned.at[pl.ds(0, count)], recv3).wait()
    result = jnp.sum(returned[...], axis=0)
    pick = lax.rem(e, 4)
    answer = result[0:3, 0:VCH]
    for t in range(1, 4):
        answer = jnp.where(pick == t, pltpu.roll(result, 128 - 32 * t, 1)[0:3, 0:VCH], answer)
    out_ref[...] = answer
    pltpu.make_async_copy(returned.at[pl.ds(0, count)], returned.at[pl.ds(0, count)], send3).wait()


def on_device(qf, qa, offset, anchor, khat, near_list, near_count, vertices):
    vmem = pl.BlockSpec(memory_space=pltpu.VMEM)
    smem = pl.BlockSpec(memory_space=pltpu.SMEM)
    dma = pltpu.SemaphoreType.DMA
    return pl.pallas_call(
        kernel,
        out_shape=jax.ShapeDtypeStruct((3, VCH), F32),
        in_specs=[vmem, vmem, vmem, smem, pl.BlockSpec(memory_space=pl.ANY), smem, smem, vmem],
        out_specs=vmem,
        scratch_shapes=[
            pltpu.VMEM((8, 128), F32),
            pltpu.VMEM((8, 128), F32),
            pltpu.VMEM((3, 8, 128), F32),
            pltpu.VMEM((8, 128), F32),
            pltpu.VMEM((2, 128), F32),
            pltpu.VMEM((24, 128), F32),
            pltpu.VMEM((NB, 8, 128), F32),
            pltpu.VMEM((NS, 2, 128), F32),
            pltpu.VMEM((3, 24, 128), F32),
            pltpu.VMEM((G, 2, G), F32),
            pltpu.VMEM((6, 256, 256), BF16),
            pltpu.VMEM((6, 256, 256), BF16),
            pltpu.VMEM((NS, 2, 128), F32),
            pltpu.VMEM((NS, 2, 128), F32),
            pltpu.VMEM((3 * NB, 5, 128, 128), F32),
            pltpu.VMEM((NB, 8, 128), F32),
            pltpu.VMEM((8, NB * B), F32),
            pltpu.VMEM((NB, 3 * NE * VCH, 128), BF16),
            pltpu.VMEM((6, 4, 128), F32),
            pltpu.VMEM((3 * NE, 4, 128), F32),
            dma(()),
            dma(()),
            dma(()),
            dma((2,)),
            dma((2,)),
            dma(()),
            dma(()),
            dma(()),
            dma(()),
        ],
        compiler_params=pltpu.CompilerParams(collective_id=0, has_side_effects=True),
    )(qf, qa, offset, anchor, khat, near_list, near_count, vertices)


def solution(mesh):
    return jax.shard_map(
        on_device,
        mesh=mesh,
        in_specs=(
            P("exc", "slab"),
            P("exc", "slab"),
            P(None, "slab"),
            P(None, "slab"),
            P(None, "slab", None),
            P("slab", None),
            P("slab"),
            P(None, "slab"),
        ),
        out_specs=P(None, ("exc", "slab")),
        check_vma=False,
    )
```

profile of v0, /device:TPU:1, one launch (start us, length us, event | category | flops | bytes accessed | tf_op | source)
XLA Modules:
  0.0 42.2 jit_solution(16138957879136241444)
XLA Ops:
  0.0 40.9 %shard_map.82 = f32[3,32]{1,0:T(4,128)} custom-call(f32[1,512]{1,0:T(1,128)} %qf_ref.1, f32[1,512]{1,0:T(1,128)} %qa_ref.1, f32[3,512]{1,0:T(4,128)} %offset_ref.1, s32[3,4]{1,0:T(4,128)} %anchor_ref.1, f32[128,2,128]{2,1,0:T(2,128)} %khat_ref.1, s32[4,8]{1,0:T(4,128)} %near_ref.1, s32[4]{0:T(128)} %count_ref.1, s32[3,512]{1,0:T(4,128)} %vertex_ref.1), custom_call_target="tpu_custom_call" | custom-call | tf_op jit(solution)/shard_map/pallas_call | solution.py:543
  40.9 1.3 %copy.10 = f32[3,32]{1,0:T(4,128)} copy(f32[3,32]{1,0:T(4,128)} %shard_map.82) | data formatting | bytes 768
where the time goes:
time: 42.3 us; the launch traced here: 42.2 us
  Pallas kernels  40.9 us (97%)
  local copies, waits for them, and re-layouts  1.26 us (3%)
    pallas_call x1, Pallas kernels, on_device(): pl.pallas_call(kernel, out_shape=jax.ShapeDtypeStruct((3, VCH), F32), in_...  40.9 us
    unnamed x1, local copies, waits for them, and re-layouts  1.26 us

commit v1 on v0

--- a/solution.py
+++ b/solution.py
@@ -87,8 +87,20 @@
     return cos_turns((c * k).astype(F32) * (1.0 / G) + shift)
 
 
+def slab_of(slot):
+    return slot % 8 * 8 + slot // 8
+
+
 def plane_of(index):
-    return jnp.where(index < 64, 2 * index, 2 * index - 127)
+    return 2 * slab_of(index % NS) + index // NS
+
+
+def below(a):
+    return jnp.concatenate([pltpu.roll(a[NS - 8 :], 1, 0), a[: NS - 8]], axis=0)
+
+
+def above(a):
+    return jnp.concatenate([a[8:], pltpu.roll(a[:8], 7, 0)], axis=0)
 
 
 def plane_tables():
@@ -117,7 +129,7 @@
     return lanes, columns, upper
 
 
-def spectrum_to_partials(xs, first_row, table_ref, split_tables, plane_fwd, plane_inv, kernel_rows, roll):
+def spectrum_to_partials(xs, first_row, split_tables, plane_fwd, plane_inv, kernel_rows):
     phases = [block_phases(xs[h], first_row) for h in range(2)]
     rows = []
     for b in range(2):
@@ -155,8 +167,8 @@
     for b in range(2):
         both = []
         for part in range(2):
-            even = planes[b][1][part] + roll(planes[b][3][part], 1, 0)
-            odd = planes[b][2][part] + roll(planes[b][0][part], NS - 1, 0)
+            even = planes[b][1][part] + below(planes[b][3][part])
+            odd = planes[b][2][part] + above(planes[b][0][part])
             both.append(jnp.concatenate([even, odd], axis=0))
         left += both
         right += [both[1], -both[0]]
@@ -180,7 +192,7 @@
         for part in range(2):
             at = slice(256 * b + 128 * part, 256 * b + 128 * part + 128)
             even, odd = back[:NS, at], back[NS:, at]
-            parts.append([roll(odd, 1, 0), even, odd, roll(even, NS - 1, 0)])
+            parts.append([below(odd), even, odd, above(even)])
         levels.append(parts)
     total = None
     for g in range(2):
@@ -232,15 +244,22 @@
 
 
 def kernel(
+    qf_hbm,
+    qa_hbm,
+    offset_hbm,
+    anchor_hbm,
+    khat_hbm,
+    near_hbm,
+    count_hbm,
+    vertex_hbm,
+    out_ref,
     qf_ref,
     qa_ref,
     offset_ref,
     anchor_ref,
-    khat_ref,
     near_ref,
     count_ref,
     vertex_ref,
-    out_ref,
     charge,
     swapped,
     offs,
@@ -276,26 +295,44 @@
     up = lax.rem(me + 1, NS)
     down = lax.rem(me + NS - 1, NS)
 
+    wx = lax.rem(me, 8)
+    y = me // 8
+    slot = 8 * wx + y
+    order = (4, 3, 5, 2, 6, 1, 7)
+    ys = [lax.rem(y + k, 8) for k in range(8)]
+    ws = [lax.rem(wx + k, 8) for k in range(8)]
+    steps = [(a, b) for a in range(8) for b in range(8) if a + b > 0]
+    steps.sort(key=lambda t: -2 * min(t[0], 8 - t[0]) - min(t[1], 8 - t[1]))
+    peers = [(8 * ys[a] + ws[b], 8 * ws[b] + ys[a]) for a, b in steps]
+
     barrier = pltpu.get_barrier_semaphore()
-
-    def greet(k, _):
-        pl.semaphore_signal(
-            barrier, inc=1, device_id=(e, lax.rem(me + k, NS)), device_id_type=MESH
+    for k in order:
+        for at in (down, up, me):
+            pl.semaphore_signal(
+                barrier, inc=1, device_id=(lax.rem(e + k, NE), at), device_id_type=MESH
+            )
+    for at, _ in peers:
+        pl.semaphore_signal(barrier, inc=1, device_id=(e, at), device_id_type=MESH)
+
+    loads = [
+        pltpu.make_async_copy(source, target, local_sem.at[n])
+        for n, (source, target) in enumerate(
+            (
+                (qf_hbm, qf_ref),
+                (qa_hbm, qa_ref),
+                (offset_hbm, offset_ref),
+                (anchor_hbm, anchor_ref),
+                (khat_hbm, khat),
+                (near_hbm, near_ref),
+                (count_hbm, count_ref),
+                (vertex_hbm, vertex_ref),
+            )
         )
-        return 0
-
-    lax.fori_loop(1, NS, greet, 0)
-
-    def greet_far(k, _):
-        other = lax.rem(e + k, NE)
-        for at in (down, me, up):
-            pl.semaphore_signal(barrier, inc=1, device_id=(other, at), device_id_type=MESH)
-        return 0
-
-    lax.fori_loop(1, NE, greet_far, 0)
-
-    kcopy = pltpu.make_async_copy(khat_ref, khat, local_sem)
-    kcopy.start()
+    ]
+    for load in loads:
+        load.start()
+    for load in loads[:4]:
+        load.wait()
 
     for g in range(2):
         for h in range(2):
@@ -319,9 +356,9 @@
     near_rows[1, :, :] = near_send[...]
     weights, slopes = [], []
     for c in range(3):
-        w, s = lagrange(offs[c])
-        weights.append(w)
-        slopes.append(s)
+        value, slope = lagrange(offs[c])
+        weights.append(value)
+        slopes.append(slope)
     value = stencil_charges(charge[...], weights)
     lane = iota((8, 128), 1)
     row = iota((8, 128), 0)
@@ -341,22 +378,19 @@
     for t in range(1, 4):
         text = text + pltpu.roll(eight[2 * t : 2 * t + 2, :], 32 * t, 1)
     message[...] = text
-    gathered[me] = text
+    gathered[slot] = text
 
     pl.semaphore_wait(barrier, NS - 1 + 3 * (NE - 1))
 
-    def send_message(k, _):
+    for at, _ in peers:
         pltpu.make_async_remote_copy(
             src_ref=message,
-            dst_ref=gathered.at[me],
+            dst_ref=gathered.at[slot],
             send_sem=send1,
             recv_sem=recv1,
-            device_id=(e, lax.rem(me + k, NS)),
+            device_id=(e, at),
             device_id_type=MESH,
         ).start()
-        return 0
-
-    lax.fori_loop(1, NS, send_message, 0)
     near_up = pltpu.make_async_remote_copy(
         src_ref=near_send,
         dst_ref=near_rows.at[0],
@@ -386,6 +420,7 @@
             table_low[3 * g + i] = low
     fwd, inv = plane_tables()
     plane_fwd, plane_inv = split(fwd), split(inv)
+    loads[7].wait()
     vertex = iota((3 * NE * VCH, 128), 0)
     for m in range(NB):
         hits = None
@@ -398,37 +433,31 @@
             hits = hit if hits is None else hits + hit
         owner[m] = hits.astype(BF16)
 
-    kcopy.wait()
+    loads[4].wait()
     kernel_rows = [khat[:, b, :] * (1.0 / (G * G * G)) for b in range(2)]
-    pltpu.make_async_copy(gathered.at[pl.ds(0, NS - 1)], gathered.at[pl.ds(0, NS - 1)], recv1).wait()
+    most = pl.ds(0, NS - 1)
+    pltpu.make_async_copy(gathered.at[most], gathered.at[most], recv1).wait()
     xs = [gathered[:, h, :] for h in range(2)]
     parts = spectrum_to_partials(
         xs,
         2 * me,
-        None,
         lambda g, i: (table_high[3 * g + i], table_low[3 * g + i]),
         plane_fwd,
         plane_inv,
         kernel_rows,
-        pltpu.roll,
     )
     for h in range(2):
         partial[:, h, :] = parts[h]
-    arrived[me] = partial[me]
-
-    def send_partial(k, _):
-        to = lax.rem(me + k, NS)
+    arrived[slot] = partial[slot]
+    for at, theirs in peers:
         pltpu.make_async_remote_copy(
-            src_ref=partial.at[to],
-            dst_ref=arrived.at[me],
+            src_ref=partial.at[theirs],
+            dst_ref=arrived.at[slot],
             send_sem=send2,
             recv_sem=recv2,
-            device_id=(e, to),
+            device_id=(e, at),
             device_id_type=MESH,
         ).start()
-        return 0
-
-    lax.fori_loop(1, NS, send_partial, 0)
 
     near_up.wait()
     near_down.wait()
@@ -438,6 +467,9 @@
             for m in range(NB):
                 at = 4 * q + m
                 spread[4 * side + m, q] = jnp.broadcast_to(columns[:, at : at + 1], (128, 128))
+
+    loads[5].wait()
+    loads[6].wait()
 
     def per_block(m, _):
         mine = own[m]
@@ -473,7 +505,7 @@
 
     lax.fori_loop(0, NB, per_block, 0)
 
-    pltpu.make_async_copy(arrived.at[pl.ds(0, NS - 1)], arrived.at[pl.ds(0, NS - 1)], recv2).wait()
+    pltpu.make_async_copy(arrived.at[most], arrived.at[most], recv2).wait()
     potential = jnp.sum(arrived[...], axis=0)
     for t in range(4):
         turned = potential if t == 0 else pltpu.roll(potential, 128 - 32 * t, 1)
@@ -501,11 +533,10 @@
         owed[t] = total[0:4, 128 * t : 128 * t + 128]
     returned[3 * e + 1] = owed[2 + e // 4]
 
-    def send_owed(k, _):
+    for k in order + (0,):
         other = lax.rem(e + k, NE)
-        for side, at in ((0, down), (1, me), (2, up)):
-
-            def start():
+        for side, at in ((0, down), (2, up), (1, me)):
+            if k > 0 or side != 1:
                 pltpu.make_async_remote_copy(
                     src_ref=owed.at[2 * side + other // 4],
                     dst_ref=returned.at[3 * e + side],
@@ -515,16 +546,8 @@
                     device_id_type=MESH,
                 ).start()
 
-            if side == 1:
-                pl.when(k > 0)(start)
-            else:
-                start()
-        return 0
-
-    lax.fori_loop(0, NE, send_owed, 0)
-
-    pltpu.make_async_copy(gathered.at[pl.ds(0, NS - 1)], gathered.at[pl.ds(0, NS - 1)], send1).wait()
-    pltpu.make_async_copy(partial.at[pl.ds(0, NS - 1)], partial.at[pl.ds(0, NS - 1)], send2).wait()
+    pltpu.make_async_copy(gathered.at[most], gathered.at[most], send1).wait()
+    pltpu.make_async_copy(partial.at[most], partial.at[most], send2).wait()
     count = 3 * NE - 1
     pltpu.make_async_copy(returned.at[pl.ds(0, count)], returned.at[pl.ds(0, count)], recv3).wait()
     result = jnp.sum(returned[...], axis=0)
@@ -538,14 +561,20 @@
 
 def on_device(qf, qa, offset, anchor, khat, near_list, near_count, vertices):
     vmem = pl.BlockSpec(memory_space=pltpu.VMEM)
-    smem = pl.BlockSpec(memory_space=pltpu.SMEM)
     dma = pltpu.SemaphoreType.DMA
     return pl.pallas_call(
         kernel,
-        out_shape=jax.ShapeDtypeStruct((3, VCH), F32),
-        in_specs=[vmem, vmem, vmem, smem, pl.BlockSpec(memory_space=pl.ANY), smem, smem, vmem],
+        out_shape=pltpu.VMEM((3, VCH), F32),
+        in_specs=[pl.BlockSpec(memory_space=pl.ANY)] * 8,
         out_specs=vmem,
         scratch_shapes=[
+            pltpu.VMEM((1, NB * B), F32),
+            pltpu.VMEM((1, NB * B), F32),
+            pltpu.VMEM((3, NB * B), F32),
+            pltpu.SMEM((3, NB), jnp.int32),
+            pltpu.SMEM((NB, MAXN), jnp.int32),
+            pltpu.SMEM((NB,), jnp.int32),
+            pltpu.VMEM((3, NB * B), jnp.int32),
             pltpu.VMEM((8, 128), F32),
             pltpu.VMEM((8, 128), F32),
             pltpu.VMEM((3, 8, 128), F32),
@@ -566,7 +595,7 @@
             pltpu.VMEM((NB, 3 * NE * VCH, 128), BF16),
             pltpu.VMEM((6, 4, 128), F32),
             pltpu.VMEM((3 * NE, 4, 128), F32),
-            dma(()),
+            dma((8,)),
             dma(()),
             dma(()),
             dma((2,)),

time: 42.3 us -> 38.8 us (0.917)
  Pallas kernels: 40.9 us -> 38.1 us
  local copies, waits for them, and re-layouts: 1.26 us -> 0.58 us
    pallas_call x1, Pallas kernels: 40.9 us -> 38.1 us  [on_device(): pl.pallas_call(kernel, out_shape=pltpu.VMEM((3, VCH), F32), in_specs=[pl....]
    unnamed x1, local copies, waits for them, and re-layouts: 1.26 us -> 0.58 us
where the time goes in v1:
time: 38.8 us; the launch traced here: 38.6 us
  Pallas kernels  38.1 us (98%)
  local copies, waits for them, and re-layouts  0.58 us (1%)
    pallas_call x1, Pallas kernels, on_device(): pl.pallas_call(kernel, out_shape=pltpu.VMEM((3, VCH), F32), in_specs=[pl....  38.1 us

profile of v1, /device:TPU:1, one launch (start us, length us, event | category | flops | bytes accessed | tf_op | source)
XLA Modules:
  0.0 38.6 jit_solution(10150101077657782366)
XLA Ops:
  0.0 38.1 %shard_map.82 = f32[3,32]{1,0:T(4,128)S(1)} custom-call(f32[1,512]{1,0:T(1,128)} %qf_hbm.1, f32[1,512]{1,0:T(1,128)} %qa_hbm.1, f32[3,512]{1,0:T(4,128)} %offset_hbm.1, s32[3,4]{1,0:T(4,128)} %anchor_hbm.1, f32[128,2,128]{2,1,0:T(2,128)} %khat_hbm.1, s32[4,8]{1,0:T(4,128)} %near_hbm.1, s32[4]{0:T(128)} %count_hbm.1, s32[3,512]{1,0:T(4,128)} %vertex_hbm.1), custom_call_target="tpu_custom_call" | custom-call | tf_op jit(solution)/shard_map/pallas_call | solution.py:565
  38.1 0.6 %copy.10 = f32[3,32]{1,0:T(4,128)} copy(f32[3,32]{1,0:T(4,128)S(1)} %shard_map.82) | data formatting | bytes 768

commit v2 on v1

--- a/solution.py
+++ b/solution.py
@@ -1,6 +1,3 @@
-import functools
-import math
-
 import jax
 import jax.numpy as jnp
 from jax import lax
@@ -20,7 +17,7 @@
 BF16 = jnp.bfloat16
 soften_sq = 16.0
 
-SIN = [(-1) ** n * (2.0 * math.pi) ** (2 * n + 1) / math.factorial(2 * n + 1) for n in range(7)]
+SIN = (6.28318516008872, -41.34165503125344, 81.60100406387009, -76.5497820930982, 39.53670463923752)
 
 
 def iota(shape, dim):
@@ -31,8 +28,8 @@
     w = t - jnp.floor(t + 0.5)
     z = 0.25 - jnp.abs(w)
     z2 = z * z
-    p = SIN[6]
-    for n in range(5, -1, -1):
+    p = SIN[4]
+    for n in range(3, -1, -1):
         p = SIN[n] + z2 * p
     return z * p
 
@@ -87,27 +84,23 @@
     return cos_turns((c * k).astype(F32) * (1.0 / G) + shift)
 
 
-def slab_of(slot):
-    return slot % 8 * 8 + slot // 8
-
-
-def plane_of(index):
-    return 2 * slab_of(index % NS) + index // NS
+def plane_of(row, base):
+    return 2 * ((base + row % NS) % NS) + row // NS
 
 
 def below(a):
-    return jnp.concatenate([pltpu.roll(a[NS - 8 :], 1, 0), a[: NS - 8]], axis=0)
+    return pltpu.roll(a, 1, 0)
 
 
 def above(a):
-    return jnp.concatenate([a[8:], pltpu.roll(a[:8], 7, 0)], axis=0)
-
-
-def plane_tables():
+    return pltpu.roll(a, NS - 1, 0)
+
+
+def plane_tables(base):
     r = iota((128, 128), 0)
     c = iota((128, 128), 1)
-    forward = (r * plane_of(c)).astype(F32) * (1.0 / G)
-    back = (plane_of(r) * c).astype(F32) * (1.0 / G)
+    forward = (r * plane_of(c, base)).astype(F32) * (1.0 / G)
+    back = (plane_of(r, base) * c).astype(F32) * (1.0 / G)
     fwd = jnp.concatenate([cos_turns(forward), sin_turns(forward)], axis=1)
     inv = jnp.concatenate([cos_turns(back), sin_turns(back)], axis=1)
     return fwd, inv
@@ -125,11 +118,11 @@
     for g in range(2):
         t = x[:, 64 * g + 29 : 64 * g + 30] * (lane.astype(F32) * (1.0 / G))
         columns.append((cos_turns(t), sin_turns(t)))
-        upper.append(jnp.broadcast_to(x[:, 64 * g + 27 : 64 * g + 28], (NS, 128)) > 0.5)
+        upper.append(jnp.broadcast_to(x[:, 64 * g + 27 : 64 * g + 28], (NS, 128)))
     return lanes, columns, upper
 
 
-def spectrum_to_partials(xs, first_row, split_tables, plane_fwd, plane_inv, kernel_rows):
+def spectrum_to_levels(xs, first_row, split_tables, plane_fwd, plane_inv, kernel_rows):
     phases = [block_phases(xs[h], first_row) for h in range(2)]
     rows = []
     for b in range(2):
@@ -151,7 +144,7 @@
         for b in range(2):
             for h in range(2):
                 cosine, sine = phases[h][1][g]
-                upper = phases[h][2][g]
+                upper = phases[h][2][g] > 0.5
                 at = slice((2 * b + h) * NS, (2 * b + h + 1) * NS)
                 v = []
                 for i in range(3):
@@ -178,8 +171,8 @@
     spectrum = dot3(plane_fwd, split(stacked))
     left, right = [], []
     for b in range(2):
-        pr = spectrum[:, 256 * b : 256 * b + 128] * kernel_rows[b]
-        pi = spectrum[:, 256 * b + 128 : 256 * b + 256] * kernel_rows[b]
+        pr = spectrum[:, 256 * b : 256 * b + 128] * kernel_rows[b, :, :]
+        pi = spectrum[:, 256 * b + 128 : 256 * b + 256] * kernel_rows[b, :, :]
         left += [pr, pi]
         right += [-pi, pr]
     stacked = jnp.concatenate(
@@ -194,26 +187,34 @@
             even, odd = back[:NS, at], back[NS:, at]
             parts.append([below(odd), even, odd, above(even)])
         levels.append(parts)
+    return phases, levels
+
+
+def levels_to_partials(phases, levels, split_tables, pick):
     total = None
     for g in range(2):
         for i in range(3):
             rows = []
             for b in range(2):
                 for h in range(2):
-                    cosine, sine = phases[h][1][g]
-                    upper = phases[h][2][g]
-                    dr, di = (jnp.where(upper, levels[b][part][i + 1], levels[b][part][i]) for part in range(2))
+                    cosine, sine = (pick(x) for x in phases[h][1][g])
+                    upper = pick(phases[h][2][g]) > 0.5
+                    dr, di = (
+                        jnp.where(upper, pick(levels[b][part][i + 1]), pick(levels[b][part][i]))
+                        for part in range(2)
+                    )
                     rows.append(
                         jnp.concatenate([dr * cosine - di * sine, dr * sine + di * cosine], axis=1)
                     )
             value = dot3(split(jnp.concatenate(rows, axis=0)), split_tables(g, i), nt=True)
             total = value if total is None else total + value
+    size = NS // 2
     out = []
     for h in range(2):
         value = None
         for b in range(2):
-            cosine, sine = phases[h][0][b]
-            at = slice((2 * b + h) * NS, (2 * b + h + 1) * NS)
+            cosine, sine = (pick(x) for x in phases[h][0][b])
+            at = slice((2 * b + h) * size, (2 * b + h + 1) * size)
             part = total[at, :128] * cosine + total[at, 128:] * sine
             value = part if value is None else value + part
         out.append(value)
@@ -270,6 +271,7 @@
     gathered,
     near_rows,
     khat,
+    kernel_rows,
     table_high,
     table_low,
     partial,
@@ -289,6 +291,7 @@
     recv2,
     send3,
     recv3,
+    ready,
 ):
     e = lax.axis_index("exc")
     me = lax.axis_index("slab")
@@ -297,22 +300,25 @@
 
     wx = lax.rem(me, 8)
     y = me // 8
-    slot = 8 * wx + y
     order = (4, 3, 5, 2, 6, 1, 7)
     ys = [lax.rem(y + k, 8) for k in range(8)]
     ws = [lax.rem(wx + k, 8) for k in range(8)]
     steps = [(a, b) for a in range(8) for b in range(8) if a + b > 0]
     steps.sort(key=lambda t: -2 * min(t[0], 8 - t[0]) - min(t[1], 8 - t[1]))
-    peers = [(8 * ys[a] + ws[b], 8 * ws[b] + ys[a]) for a, b in steps]
+    peers = [(8 * ys[a] + ws[b], 8 * a + ws[b], 8 * ((8 - a) % 8) + wx) for a, b in steps]
+    far_peers = [p for p, (a, b) in zip(peers, steps) if 2 <= a < 6]
+    close_peers = [p for p, (a, b) in zip(peers, steps) if not 2 <= a < 6]
 
     barrier = pltpu.get_barrier_semaphore()
-    for k in order:
-        for at in (down, up, me):
-            pl.semaphore_signal(
-                barrier, inc=1, device_id=(lax.rem(e + k, NE), at), device_id_type=MESH
-            )
-    for at, _ in peers:
+    for at, _, _ in peers:
         pl.semaphore_signal(barrier, inc=1, device_id=(e, at), device_id_type=MESH)
+
+    for other in range(1, NE):
+
+        @pl.when(other > e)
+        def _():
+            for at in (down, up, me):
+                pl.semaphore_signal(barrier, inc=1, device_id=(other, at), device_id_type=MESH)
 
     loads = [
         pltpu.make_async_copy(source, target, local_sem.at[n])
@@ -378,14 +384,14 @@
     for t in range(1, 4):
         text = text + pltpu.roll(eight[2 * t : 2 * t + 2, :], 32 * t, 1)
     message[...] = text
-    gathered[slot] = text
-
-    pl.semaphore_wait(barrier, NS - 1 + 3 * (NE - 1))
-
-    for at, _ in peers:
+    gathered[wx] = text
+
+    pl.semaphore_wait(barrier, NS - 1 + 3 * e)
+
+    for at, _, there in peers:
         pltpu.make_async_remote_copy(
             src_ref=message,
-            dst_ref=gathered.at[slot],
+            dst_ref=gathered.at[there],
             send_sem=send1,
             recv_sem=recv1,
             device_id=(e, at),
@@ -409,6 +415,12 @@
     )
     near_up.start()
     near_down.start()
+    for other in range(NE - 1):
+
+        @pl.when(other < e)
+        def _():
+            for at in (down, up, me):
+                pl.semaphore_signal(ready, inc=1, device_id=(other, at), device_id_type=MESH)
 
     base = lane_tables()
     lanes = iota((256, 256), 0) % 128
@@ -418,7 +430,7 @@
             high, low = split(jnp.where(mine, base, 0.0))
             table_high[3 * g + i] = high
             table_low[3 * g + i] = low
-    fwd, inv = plane_tables()
+    fwd, inv = plane_tables(8 * y)
     plane_fwd, plane_inv = split(fwd), split(inv)
     loads[7].wait()
     vertex = iota((3 * NE * VCH, 128), 0)
@@ -434,30 +446,45 @@
         owner[m] = hits.astype(BF16)
 
     loads[4].wait()
-    kernel_rows = [khat[:, b, :] * (1.0 / (G * G * G)) for b in range(2)]
+    for b in range(2):
+        kernel_rows[b] = khat[:, b, :] * (1.0 / (G * G * G))
     most = pl.ds(0, NS - 1)
     pltpu.make_async_copy(gathered.at[most], gathered.at[most], recv1).wait()
     xs = [gathered[:, h, :] for h in range(2)]
-    parts = spectrum_to_partials(
-        xs,
-        2 * me,
-        lambda g, i: (table_high[3 * g + i], table_low[3 * g + i]),
-        plane_fwd,
-        plane_inv,
-        kernel_rows,
+    def split_tables(g, i):
+        return table_high[3 * g + i], table_low[3 * g + i]
+
+    phases, levels = spectrum_to_levels(
+        xs, 2 * me, split_tables, plane_fwd, plane_inv, kernel_rows
     )
+
+    def send_partials(to):
+        for at, here, there in to:
+            pltpu.make_async_remote_copy(
+                src_ref=partial.at[here],
+                dst_ref=arrived.at[there],
+                send_sem=send2,
+                recv_sem=recv2,
+                device_id=(e, at),
+                device_id_type=MESH,
+            ).start()
+
+    parts = levels_to_partials(phases, levels, split_tables, lambda x: x[16:48])
     for h in range(2):
-        partial[:, h, :] = parts[h]
-    arrived[slot] = partial[slot]
-    for at, theirs in peers:
-        pltpu.make_async_remote_copy(
-            src_ref=partial.at[theirs],
-            dst_ref=arrived.at[slot],
-            send_sem=send2,
-            recv_sem=recv2,
-            device_id=(e, at),
-            device_id_type=MESH,
-        ).start()
+        partial[16:48, h, :] = parts[h]
+    send_partials(far_peers)
+
+    @pl.when(me >= 0)
+    def _():
+        parts = levels_to_partials(
+            phases, levels, split_tables, lambda x: jnp.concatenate([x[48:], x[:16]], axis=0)
+        )
+        for h in range(2):
+            partial[48:64, h, :] = parts[h][:16]
+            partial[0:16, h, :] = parts[h][16:]
+
+    arrived[wx] = partial[wx]
+    send_partials(close_peers)
 
     near_up.wait()
     near_down.wait()
@@ -529,16 +556,28 @@
         low, last = split(whole - high.astype(F32))
         got = dot(high, owner[m], nt=True) + (dot(low, owner[m], nt=True) + dot(last, owner[m], nt=True))
         total = got if total is None else total + got
+    row = iota((8, 128), 0)
+    diagonal = iota((8, 128), 1) // VCH == row
     for t in range(6):
-        owed[t] = total[0:4, 128 * t : 128 * t + 128]
-    returned[3 * e + 1] = owed[2 + e // 4]
+        tile = total[:, 128 * t : 128 * t + 128]
+        turns = [tile] + [pltpu.roll(tile, VCH * d, 1) for d in range(1, 4)]
+        for part in range(4):
+            line = jnp.zeros((8, 128), F32)
+            for c in range(3):
+                line = jnp.where(diagonal & (row == c), turns[(c - part) % 4], line)
+            owed[4 * t + part] = jnp.sum(line, axis=0, keepdims=True)
+    returned[3 * e + 1] = owed[NE + e]
+
+    @pl.when(e < NE - 1)
+    def _():
+        pl.semaphore_wait(ready, 3 * (NE - 1 - e))
 
     for k in order + (0,):
         other = lax.rem(e + k, NE)
         for side, at in ((0, down), (2, up), (1, me)):
             if k > 0 or side != 1:
                 pltpu.make_async_remote_copy(
-                    src_ref=owed.at[2 * side + other // 4],
+                    src_ref=owed.at[NE * side + other],
                     dst_ref=returned.at[3 * e + side],
                     send_sem=send3,
                     recv_sem=recv3,
@@ -551,11 +590,9 @@
     count = 3 * NE - 1
     pltpu.make_async_copy(returned.at[pl.ds(0, count)], returned.at[pl.ds(0, count)], recv3).wait()
     result = jnp.sum(returned[...], axis=0)
-    pick = lax.rem(e, 4)
-    answer = result[0:3, 0:VCH]
-    for t in range(1, 4):
-        answer = jnp.where(pick == t, pltpu.roll(result, 128 - 32 * t, 1)[0:3, 0:VCH], answer)
-    out_ref[...] = answer
+    out_ref[0:1, :] = result[:, 0:VCH]
+    for c in range(1, 3):
+        out_ref[c : c + 1, :] = pltpu.roll(result, 128 - VCH * c, 1)[:, 0:VCH]
     pltpu.make_async_copy(returned.at[pl.ds(0, count)], returned.at[pl.ds(0, count)], send3).wait()
 
 
@@ -585,6 +622,7 @@
             pltpu.VMEM((NS, 2, 128), F32),
             pltpu.VMEM((3, 24, 128), F32),
             pltpu.VMEM((G, 2, G), F32),
+            pltpu.VMEM((2, G, G), F32),
             pltpu.VMEM((6, 256, 256), BF16),
             pltpu.VMEM((6, 256, 256), BF16),
             pltpu.VMEM((NS, 2, 128), F32),
@@ -593,8 +631,8 @@
             pltpu.VMEM((NB, 8, 128), F32),
             pltpu.VMEM((8, NB * B), F32),
             pltpu.VMEM((NB, 3 * NE * VCH, 128), BF16),
-            pltpu.VMEM((6, 4, 128), F32),
-            pltpu.VMEM((3 * NE, 4, 128), F32),
+            pltpu.VMEM((3 * NE, 1, 128), F32),
+            pltpu.VMEM((3 * NE, 1, 128), F32),
             dma((8,)),
             dma(()),
             dma(()),
@@ -604,6 +642,7 @@
             dma(()),
             dma(()),
             dma(()),
+            pltpu.SemaphoreType.REGULAR,
         ],
         compiler_params=pltpu.CompilerParams(collective_id=0, has_side_effects=True),
     )(qf, qa, offset, anchor, khat, near_list, near_count, vertices)

time: 38.8 us -> 38 us (0.979)
  Pallas kernels: 38.1 us -> 37.3 us
    pallas_call x1, Pallas kernels: 38.1 us -> 37.3 us  [on_device(): pl.pallas_call(kernel, out_shape=pltpu.VMEM((3, VCH), F32), in_specs=[pl....]
where the time goes in v2:
time: 38 us; the launch traced here: 37.9 us
  Pallas kernels  37.3 us (98%)
  local copies, waits for them, and re-layouts  0.58 us (2%)
    pallas_call x1, Pallas kernels, on_device(): pl.pallas_call(kernel, out_shape=pltpu.VMEM((3, VCH), F32), in_specs=[pl....  37.3 us

profile of v2, /device:TPU:1, one launch (start us, length us, event | category | flops | bytes accessed | tf_op | source)
XLA Modules:
  0.0 37.9 jit_solution(12746943398323327110)
XLA Ops:
  0.0 37.3 %shard_map.82 = f32[3,32]{1,0:T(4,128)S(1)} custom-call(f32[1,512]{1,0:T(1,128)} %qf_hbm.1, f32[1,512]{1,0:T(1,128)} %qa_hbm.1, f32[3,512]{1,0:T(4,128)} %offset_hbm.1, s32[3,4]{1,0:T(4,128)} %anchor_hbm.1, f32[128,2,128]{2,1,0:T(2,128)} %khat_hbm.1, s32[4,8]{1,0:T(4,128)} %near_hbm.1, s32[4]{0:T(128)} %count_hbm.1, s32[3,512]{1,0:T(4,128)} %vertex_hbm.1), custom_call_target="tpu_custom_call" | custom-call | tf_op jit(solution)/shard_map/pallas_call | solution.py:602
  37.3 0.6 %copy.10 = f32[3,32]{1,0:T(4,128)} copy(f32[3,32]{1,0:T(4,128)S(1)} %shard_map.82) | data formatting | bytes 768
